TPU v7x, 128 devices: a whole 4x4x4 slice. The times are simulated.
128 devices in a mesh: pairs: 64 (over x, z, y), comp: 2 (over core).
Axes of the slice: x: 4, y: 4, z: 4, core: 2. Of those that a mesh axis runs over, the one named last changes fastest.
Arguments:
- effects: float32 [49, 524288], P(None, 'pairs'), may hold values from -24 to 24
- se_table: float32 [16, 49], replicated, may hold values from 0.5 to 2
- se_index: int32 [1024], P('pairs'), may hold values from 0 to 15
- base_root: float32 [16, 49, 49], replicated, may hold values from -0.875 to 0.875
- grid_scale: float32 [16], replicated, may hold values from 0.25 to 4
- comp_base: int32 [256], P('comp'), may hold values from 0 to 15
- comp_grid: int32 [256], P('comp'), may hold values from 0 to 15
- weights: float32 [256], P('comp'), may hold values from 0.2 to 5
Outputs:
- responsibility: float32 [256, 524288], P('comp', 'pairs')
- log_weights: float32 [256], P('comp')
- pair_loglik: float32 [524288], P('pairs')
All inputs are finite; a program needn't handle non-finite values.
Results may differ from a plain program's by a relative error of at most 0.0003.
Values sent between devices are 32-bit elements; how exact they have to be, the bound alone decides.
A program may use at most 384 MiB of HBM per device.

v0:
```python
import math

import jax
import jax.numpy as jnp
from jax import lax
from jax.sharding import PartitionSpec as P

TILE = 512


def sent_to_all(array, axis):
    count = lax.axis_size(axis)
    return lax.all_to_all(
        jnp.broadcast_to(array[None], (count, *array.shape)), axis, 0, 0, tiled=True
    )


def over_copies(array, axis):
    everything = sent_to_all(array, axis)
    return jnp.sum(everything, axis=0)


def build_factors(se_rows, covar_rows, scale_rows):
    tissues = se_rows.shape[1]
    identity = jnp.eye(tissues, dtype=jnp.float32)
    system = (scale_rows * scale_rows)[:, None, None] * covar_rows.reshape(-1, tissues, tissues)
    system = system + identity[None] * (se_rows * se_rows)[:, :, None]
    factor = jnp.linalg.cholesky(system)
    eye_full = jnp.broadcast_to(identity, factor.shape)
    inverse = jax.scipy.linalg.solve_triangular(factor, eye_full, lower=True)
    logdet = jnp.sum(jnp.log(jnp.diagonal(factor, axis1=1, axis2=2)), axis=1)
    return (inverse, logdet)


def exact_dot(left, right):
    return jnp.dot(left, right, precision=lax.Precision.HIGHEST, preferred_element_type=jnp.float32)


def per_device(effects, se_table, se_index, base_root, grid_scale, comp_base, comp_grid, weights):
    tissues = effects.shape[0]
    local_pairs = effects.shape[1]
    comp_count = comp_base.shape[0]
    block_count = se_table.shape[0]
    covariances = jnp.einsum("uij,ukj->uik", base_root, base_root, precision=lax.Precision.HIGHEST)
    covariances = covariances.reshape(covariances.shape[0], tissues * tissues)
    base_pick = (
        comp_base[:, None] == jnp.arange(covariances.shape[0], dtype=jnp.int32)[None]
    ).astype(jnp.float32)
    comp_covar = exact_dot(base_pick, covariances)
    grid_pick = (
        comp_grid[:, None] == jnp.arange(grid_scale.shape[0], dtype=jnp.int32)[None]
    ).astype(jnp.float32)
    comp_scale = exact_dot(grid_pick, grid_scale)
    item_share = block_count * comp_count // lax.axis_size("pairs")
    item_first = lax.axis_index("pairs") * item_share
    item_ids = item_first + jnp.arange(item_share, dtype=jnp.int32)
    block_pick = (
        (item_ids // comp_count)[:, None] == jnp.arange(block_count, dtype=jnp.int32)[None]
    ).astype(jnp.float32)
    item_pick = (
        (item_ids % comp_count)[:, None] == jnp.arange(comp_count, dtype=jnp.int32)[None]
    ).astype(jnp.float32)
    own_inverse, own_logdet = build_factors(
        exact_dot(block_pick, se_table),
        exact_dot(item_pick, comp_covar),
        exact_dot(item_pick, comp_scale),
    )
    inverse, logdet = (
        lax.all_gather(own_inverse, "pairs", axis=0, tiled=True),
        lax.all_gather(own_logdet, "pairs", axis=0, tiled=True),
    )
    whiten_table = inverse.reshape(block_count, comp_count, tissues, tissues).transpose(0, 3, 2, 1)
    whiten_table = whiten_table.reshape(block_count, tissues, tissues * comp_count)
    logdet_table = logdet.reshape(block_count, comp_count)
    log_prior = jnp.log(weights)
    constant = 0.5 * tissues * math.log(2.0 * math.pi)

    def one_tile(tile_id, scores):
        block_id = se_index[tile_id]
        block_table = lax.dynamic_index_in_dim(whiten_table, block_id, 0, keepdims=False)
        tile_data = lax.dynamic_slice_in_dim(effects, tile_id * TILE, TILE, 1)
        whitened = lax.dot_general(
            block_table,
            tile_data,
            (((0,), (0,)), ((), ())),
            precision=lax.Precision.HIGHEST,
            preferred_element_type=jnp.float32,
        )
        whitened = whitened.reshape(tissues, comp_count, TILE)
        quadratic = jnp.sum(whitened * whitened, axis=0)
        logdet_row = lax.dynamic_index_in_dim(logdet_table, block_id, 0, keepdims=False)
        tile_scores = log_prior[:, None] - 0.5 * quadratic - logdet_row[:, None] - constant
        return lax.dynamic_update_slice_in_dim(scores, tile_scores, tile_id * TILE, 1)

    scores = lax.fori_loop(
        0, local_pairs // TILE, one_tile, jnp.zeros((comp_count, local_pairs), jnp.float32)
    )
    local_max = jnp.max(scores, axis=0)
    score_max = lax.pmax(local_max, "comp")
    score_sum = lax.psum(jnp.sum(jnp.exp(scores - score_max), axis=0), "comp")
    pair_loglik = score_max + jnp.log(score_sum)
    responsibility = jnp.exp(scores - pair_loglik)
    masses = over_copies(jnp.sum(responsibility, axis=1), "pairs")
    all_pairs = local_pairs * lax.axis_size("pairs")
    all_comps = comp_count * lax.axis_size("comp")
    log_weights = jnp.log((masses + 1.0) / (all_pairs + all_comps))
    return (responsibility, log_weights, pair_loglik)


def solution(mesh):
    placed = (P(None, "pairs"), P(), P("pairs"), P(), P(), P("comp"), P("comp"), P("comp"))
    return jax.shard_map(
        per_device,
        mesh=mesh,
        in_specs=placed,
        out_specs=(P("comp", "pairs"), P("comp"), P("pairs")),
        check_vma=False,
    )
```

profile of v0, /device:TPU:0, one launch (start us, length us, event | category | flops | bytes accessed | tf_op | source)
XLA Modules:
  0.0 874.1 jit_solution(2384535408686708736)
XLA Ops:
  14.2 143.6 %custom-call.8 = f32[32,49,49]{2,1,0:T(8,128)S(1)} custom-call(f32[32,49,49]{2,1,0:T(8,128)S(1)} %fusion.6), custom_call_target="Cholesky" | custom-call | tf_op jit(solution)/shard_map/jit(cholesky)/cholesky | solution.py:28
  160.6 38.6 %custom-call.9 = f32[32,1,49,49]{0,2,3,1:T(8,128)} custom-call(f32[32,1,49,49]{0,3,2,1:T(8,128)} %get-tuple-element.224), custom_call_target="InvertDiagBlocksLowerTriangular" | custom-call | tf_op jit(solution)/shard_map/jit(_solve_triangular)/vmap()/triangular_solve | solution.py:30
  206.4 190.0 %all-reduce = f32[2048]{0:T(1024)S(1)} all-reduce(f32[2048]{0:T(1024)S(1)} %dynamic-update-slice.3), channel_id=1, replica_groups=mesh['pairs'=64,'comp'=2] {'pairs'}, use_global_device_ids=true, to_apply=%add | all-reduce | flops 2048 | bytes 16384
  396.4 57.9 %all-gather.2.cloned.1.call-done = f32[2048,49,49]{2,0,1:T(8,128)} async-done(((f32[32,49,49]{2,0,1:T(8,128)}), f32[2048,49,49]{2,0,1:T(8,128)}) %all-gather.2.cloned.1.call-update) | async-done | bytes 19669008 | tf_op jit(solution)/shard_map/all_gather | solution.py:69
  454.3 39.8 %copy.69 = f32[16,128,49,49]{1,2,0,3:T(8,128)} copy(f32[16,128,49,49]{3,1,0,2:T(8,128)} %bitcast.54) | data formatting | bytes 39337984 | tf_op jit(solution)/shard_map/reshape | solution.py:72
  494.1 22.4 %reshape.99 = f32[16,49,6272]{2,0,1:T(8,128)} reshape(f32[16,49,49,128]{3,2,0,1:T(8,128)} %bitcast.53) | data formatting | bytes 39337984 | tf_op jit(solution)/shard_map/reshape | solution.py:73
  518.9 314.0 %while.15 = (s32[]{:T(128)}, f32[128,8192]{1,0:T(8,128)}, f32[128]{0:T(128)S(1)}, s32[16]{0:T(128)S(1)}, f32[16,49,6272]{2,0,1:T(8,128)}, /*index=5*/f32[49,8192...) while((s32[]{:T(128)}, f32[128,8192]{1,0:T(8,128)}, ...), condition=%wide.region_5.6_spmd, body=%wide.region_3.5_spmd.sunk | while | flops 1894842368 | bytes 9508577 | solution.py:95
  526.4 11.3 %multiply_reduce_fusion.2 = f32[128,512]{1,0:T(8,128)S(1)} fusion(f32[49,128,49]{1,0,2:T(8,128)S(1)} %dot_general.34, f32[49,8192]{1,0:T(8,128)} %get-tuple-element.300, s32[]{:T(128)S(6)} %select_n.69), kind=kOutput, calls=%fused_computation.1.clone.1 | convolution fusion | flops 1894580224 | bytes 1606148 | tf_op jit(solution)/shard_map/while/body/eval_jaxpr/dot_general | solution.py:82
  541.0 4.7 constant_dynamic-slice_fusion.3
  546.0 11.3 %multiply_reduce_fusion.2 = f32[128,512]{1,0:T(8,128)S(1)} fusion(f32[49,128,49]{1,0,2:T(8,128)S(1)} %dot_general.34, f32[49,8192]{1,0:T(8,128)} %get-tuple-element.300, s32[]{:T(128)S(6)} %select_n.69), kind=kOutput, calls=%fused_computation.1.clone.1 | convolution fusion | flops 1894580224 | bytes 1606148 | tf_op jit(solution)/shard_map/while/body/eval_jaxpr/dot_general | solution.py:82
  565.6 11.3 %multiply_reduce_fusion.2 = f32[128,512]{1,0:T(8,128)S(1)} fusion(f32[49,128,49]{1,0,2:T(8,128)S(1)} %dot_general.34, f32[49,8192]{1,0:T(8,128)} %get-tuple-element.300, s32[]{:T(128)S(6)} %select_n.69), kind=kOutput, calls=%fused_computation.1.clone.1 | convolution fusion | flops 1894580224 | bytes 1606148 | tf_op jit(solution)/shard_map/while/body/eval_jaxpr/dot_general | solution.py:82
  580.3 4.7 constant_dynamic-slice_fusion.3
  585.3 11.3 %multiply_reduce_fusion.2 = f32[128,512]{1,0:T(8,128)S(1)} fusion(f32[49,128,49]{1,0,2:T(8,128)S(1)} %dot_general.34, f32[49,8192]{1,0:T(8,128)} %get-tuple-element.300, s32[]{:T(128)S(6)} %select_n.69), kind=kOutput, calls=%fused_computation.1.clone.1 | convolution fusion | flops 1894580224 | bytes 1606148 | tf_op jit(solution)/shard_map/while/body/eval_jaxpr/dot_general | solution.py:82
  599.9 4.7 constant_dynamic-slice_fusion.3
  604.9 11.3 %multiply_reduce_fusion.2 = f32[128,512]{1,0:T(8,128)S(1)} fusion(f32[49,128,49]{1,0,2:T(8,128)S(1)} %dot_general.34, f32[49,8192]{1,0:T(8,128)} %get-tuple-element.300, s32[]{:T(128)S(6)} %select_n.69), kind=kOutput, calls=%fused_computation.1.clone.1 | convolution fusion | flops 1894580224 | bytes 1606148 | tf_op jit(solution)/shard_map/while/body/eval_jaxpr/dot_general | solution.py:82
  619.6 4.7 constant_dynamic-slice_fusion.3
  624.5 11.3 %multiply_reduce_fusion.2 = f32[128,512]{1,0:T(8,128)S(1)} fusion(f32[49,128,49]{1,0,2:T(8,128)S(1)} %dot_general.34, f32[49,8192]{1,0:T(8,128)} %get-tuple-element.300, s32[]{:T(128)S(6)} %select_n.69), kind=kOutput, calls=%fused_computation.1.clone.1 | convolution fusion | flops 1894580224 | bytes 1606148 | tf_op jit(solution)/shard_map/while/body/eval_jaxpr/dot_general | solution.py:82
  639.2 4.7 constant_dynamic-slice_fusion.3
  644.2 11.3 %multiply_reduce_fusion.2 = f32[128,512]{1,0:T(8,128)S(1)} fusion(f32[49,128,49]{1,0,2:T(8,128)S(1)} %dot_general.34, f32[49,8192]{1,0:T(8,128)} %get-tuple-element.300, s32[]{:T(128)S(6)} %select_n.69), kind=kOutput, calls=%fused_computation.1.clone.1 | convolution fusion | flops 1894580224 | bytes 1606148 | tf_op jit(solution)/shard_map/while/body/eval_jaxpr/dot_general | solution.py:82
  663.8 11.3 %multiply_reduce_fusion.2 = f32[128,512]{1,0:T(8,128)S(1)} fusion(f32[49,128,49]{1,0,2:T(8,128)S(1)} %dot_general.34, f32[49,8192]{1,0:T(8,128)} %get-tuple-element.300, s32[]{:T(128)S(6)} %select_n.69), kind=kOutput, calls=%fused_computation.1.clone.1 | convolution fusion | flops 1894580224 | bytes 1606148 | tf_op jit(solution)/shard_map/while/body/eval_jaxpr/dot_general | solution.py:82
  683.4 11.3 %multiply_reduce_fusion.2 = f32[128,512]{1,0:T(8,128)S(1)} fusion(f32[49,128,49]{1,0,2:T(8,128)S(1)} %dot_general.34, f32[49,8192]{1,0:T(8,128)} %get-tuple-element.300, s32[]{:T(128)S(6)} %select_n.69), kind=kOutput, calls=%fused_computation.1.clone.1 | convolution fusion | flops 1894580224 | bytes 1606148 | tf_op jit(solution)/shard_map/while/body/eval_jaxpr/dot_general | solution.py:82
  703.0 11.3 %multiply_reduce_fusion.2 = f32[128,512]{1,0:T(8,128)S(1)} fusion(f32[49,128,49]{1,0,2:T(8,128)S(1)} %dot_general.34, f32[49,8192]{1,0:T(8,128)} %get-tuple-element.300, s32[]{:T(128)S(6)} %select_n.69), kind=kOutput, calls=%fused_computation.1.clone.1 | convolution fusion | flops 1894580224 | bytes 1606148 | tf_op jit(solution)/shard_map/while/body/eval_jaxpr/dot_general | solution.py:82
  722.6 11.3 %multiply_reduce_fusion.2 = f32[128,512]{1,0:T(8,128)S(1)} fusion(f32[49,128,49]{1,0,2:T(8,128)S(1)} %dot_general.34, f32[49,8192]{1,0:T(8,128)} %get-tuple-element.300, s32[]{:T(128)S(6)} %select_n.69), kind=kOutput, calls=%fused_computation.1.clone.1 | convolution fusion | flops 1894580224 | bytes 1606148 | tf_op jit(solution)/shard_map/while/body/eval_jaxpr/dot_general | solution.py:82
  737.3 4.7 constant_dynamic-slice_fusion.3
  742.3 11.3 %multiply_reduce_fusion.2 = f32[128,512]{1,0:T(8,128)S(1)} fusion(f32[49,128,49]{1,0,2:T(8,128)S(1)} %dot_general.34, f32[49,8192]{1,0:T(8,128)} %get-tuple-element.300, s32[]{:T(128)S(6)} %select_n.69), kind=kOutput, calls=%fused_computation.1.clone.1 | convolution fusion | flops 1894580224 | bytes 1606148 | tf_op jit(solution)/shard_map/while/body/eval_jaxpr/dot_general | solution.py:82
  761.9 11.3 %multiply_reduce_fusion.2 = f32[128,512]{1,0:T(8,128)S(1)} fusion(f32[49,128,49]{1,0,2:T(8,128)S(1)} %dot_general.34, f32[49,8192]{1,0:T(8,128)} %get-tuple-element.300, s32[]{:T(128)S(6)} %select_n.69), kind=kOutput, calls=%fused_computation.1.clone.1 | convolution fusion | flops 1894580224 | bytes 1606148 | tf_op jit(solution)/shard_map/while/body/eval_jaxpr/dot_general | solution.py:82
  781.5 11.3 %multiply_reduce_fusion.2 = f32[128,512]{1,0:T(8,128)S(1)} fusion(f32[49,128,49]{1,0,2:T(8,128)S(1)} %dot_general.34, f32[49,8192]{1,0:T(8,128)} %get-tuple-element.300, s32[]{:T(128)S(6)} %select_n.69), kind=kOutput, calls=%fused_computation.1.clone.1 | convolution fusion | flops 1894580224 | bytes 1606148 | tf_op jit(solution)/shard_map/while/body/eval_jaxpr/dot_general | solution.py:82
  796.2 4.7 constant_dynamic-slice_fusion.3
  801.1 11.3 %multiply_reduce_fusion.2 = f32[128,512]{1,0:T(8,128)S(1)} fusion(f32[49,128,49]{1,0,2:T(8,128)S(1)} %dot_general.34, f32[49,8192]{1,0:T(8,128)} %get-tuple-element.300, s32[]{:T(128)S(6)} %select_n.69), kind=kOutput, calls=%fused_computation.1.clone.1 | convolution fusion | flops 1894580224 | bytes 1606148 | tf_op jit(solution)/shard_map/while/body/eval_jaxpr/dot_general | solution.py:82
  820.8 11.3 %multiply_reduce_fusion.2 = f32[128,512]{1,0:T(8,128)S(1)} fusion(f32[49,128,49]{1,0,2:T(8,128)S(1)} %dot_general.34, f32[49,8192]{1,0:T(8,128)} %get-tuple-element.300, s32[]{:T(128)S(6)} %select_n.69), kind=kOutput, calls=%fused_computation.1.clone.1 | convolution fusion | flops 1894580224 | bytes 1606148 | tf_op jit(solution)/shard_map/while/body/eval_jaxpr/dot_general | solution.py:82
  845.2 4.8 fusion.20
  850.0 16.7 %all_to_all.6 = f32[64,1,128]{2,1,0:T(1,128)S(1)} all-to-all(f32[64,1,128]{2,1,0:T(1,128)S(1)} %broadcast_in_dim.13), channel_id=1, replica_groups=mesh['pairs'=64,'comp'=2] {'pairs'}, dimensions={0} | all-to-all | bytes 65536 | tf_op jit(solution)/shard_map/all_to_all | solution.py:13
  (149 shorter events, 100.5 us)
Async XLA Ops:
  7.2 5.9 copy-start
  7.2 2.5 copy-start.3
  7.2 447.1 %all-gather.2.cloned.1.call-start = ((), (), s32[]{:S(2)}) async-start(), calls=%async_computation.1 | async-start | bytes 52183040 | tf_op jit(solution)/shard_map/all_gather | solution.py:69
  11.7 0.8 copy-start.4
  11.7 0.8 copy-start.5
  202.7 1.1 copy-start.6
  202.7 2.1 copy-start.8
  516.4 2.5 copy-start.7
  845.1 4.8 copy-start.2
  845.2 22.1 %copy-start.1 = (f32[16,49]{1,0:T(8,128)S(1)}, f32[16,49]{1,0:T(8,128)}, u32[]{:S(2)}) copy-start(f32[16,49]{1,0:T(8,128)} %param.11) | copy-start | bytes 9412
Sparse Core Ops, SparseCore 0:
  203.9 250.3 all-gather.1
where the time goes:
time: 877 us; the launch traced here: 874 us
  blocking collectives  214 us (24%)
  other arithmetic  209 us (24%)
  matrix products  187 us (21%)
  local copies, waits for them, and re-layouts  160 us (18%)
  waiting for transfers between devices  57.9 us (7%)
  loops' own time  31.8 us (4%)
  between operations  15 us (2%)
    unnamed x1, blocking collectives  190 us
    dot_general x16, matrix products, one_tile(): lax.dot_general(block_table, tile_data, (((0,), (0,)), ((), ())), precisi...  180 us
    another operation x4, other arithmetic, build_factors(): factor = jnp.linalg.cholesky(system)  144 us
    dynamic_slice x32, local copies, waits for them, and re-layouts, one_tile(): lax.dynamic_index_in_dim(whiten_table, block_id, 0, keepdims=False)  76.1 us
    all_gather x1, waiting for transfers between devices, per_device(): lax.all_gather(own_inverse, 'pairs', axis=0, tiled=True)  57.9 us
    another operation x3, other arithmetic, build_factors(): inverse = jax.scipy.linalg.solve_triangular(factor, eye_full, lower=True)  40.1 us
    reshape x1, local copies, waits for them, and re-layouts, per_device(): inverse.reshape(block_count, comp_count, tissues, tissues)  39.8 us
    another operation x1, loops' own time, per_device(): lax.fori_loop(0, local_pairs // TILE, one_tile, jnp.zeros((comp_count, lo...  31.8 us
  transfers between devices with their start and end apart: 1, of which 1 were waited for; matrix products, arithmetic and copies ran while one was open for 0% of the time, Pallas kernels for 0%

commit v1 on v0

v1 whole, which is shorter than its diff:
```python
import math

import jax
import jax.numpy as jnp
from jax import lax
from jax.experimental import pallas as pl
from jax.experimental.pallas import tpu as pltpu
from jax.sharding import PartitionSpec as P

TILE = 512
R = 49
NBLK = 6
FEATS = 1280
OFF_BORDER = 960
OFF_LAST = 1008
OFF_DIAG = 1016
OFF_BIAS = 1256
HIGHEST = lax.Precision.HIGHEST


def row8(index):
    return pl.ds(pl.multiple_of(index * 8, 8), 8)


def invert_all(covar_ref, se2_ref, prior_ref, w_ref, d_ref, b_ref, c_ref, v_ref, x_ref):
    def w_at(g, f):
        return row8(g * FEATS + f)

    def d_at(g, block, a, c):
        return row8((g * NBLK + block) * 64 + a * 8 + c)

    def p_at(g, block, a, c):
        return row8((g * NBLK + block) * 64 + a * 8 + c)

    def pair_base(i, j):
        return (i * (i - 1) // 2 + j) * 64

    def cov(i, j):
        return jnp.broadcast_to(covar_ref[i, pl.ds(j, 1), :], (8, 128))

    def x_at(g, n):
        return row8(g * 72 + n)

    for g in range(2):
        se_last = se2_ref[48, g * 8 : g * 8 + 8, :]
        pivot = cov(48, 48) + se_last
        inv = 1.0 / pivot
        x_ref[x_at(g, 48), :] = jnp.log(pivot)
        w_ref[w_at(g, OFF_LAST), :] = -inv
        for i in range(48):
            edge = cov(48, i)
            x_ref[x_at(g, i), :] = edge
            w_ref[w_at(g, OFF_BORDER + i), :] = edge * inv

    def init_group(g, _):
        def init_row(i, _):
            edges = [x_ref[x_at(g, i * 8 + a), :] for a in range(8)]

            def init_pair(j, _):
                scaled = [w_ref[w_at(g, OFF_BORDER + j * 8 + c), :] for c in range(8)]
                base = pair_base(i, j)
                for a in range(8):
                    for c in range(8):
                        w_ref[w_at(g, base + a * 8 + c), :] = cov(i * 8 + a, j * 8 + c) - edges[a] * scaled[c]
                return 0

            lax.fori_loop(0, i, init_pair, 0)
            scaled = [w_ref[w_at(g, OFF_BORDER + i * 8 + c), :] for c in range(8)]
            for a in range(8):
                for c in range(a + 1):
                    entry = cov(i * 8 + a, i * 8 + c) - edges[a] * scaled[c]
                    if a == c:
                        entry = entry + se2_ref[i * 8 + a, pl.ds(pl.multiple_of(g * 8, 8), 8), :]
                    d_ref[d_at(g, i, a, c), :] = entry
            return 0

        lax.fori_loop(0, NBLK, init_row, 0)
        return 0

    lax.fori_loop(0, 2, init_group, 0)

    def pivot_block(k):
        for g in range(2):
            m = {(a, c): d_ref[d_at(g, k, a, c), :] for a in range(8) for c in range(a + 1)}
            product = None
            for s in range(8):
                p = m[s, s]
                product = p if product is None else product * p
                inv = 1.0 / p
                col = {a: (m[a, s] if a > s else m[s, a]) for a in range(8) if a != s}
                scaled = {a: col[a] * inv for a in col}
                for a in col:
                    for c in col:
                        if c <= a:
                            m[a, c] = m[a, c] - scaled[a] * col[c]
                for a in col:
                    m[max(a, s), min(a, s)] = scaled[a]
                m[s, s] = -inv
            x_ref[x_at(g, 48), :] = x_ref[x_at(g, 48), :] + jnp.log(product)
            for a in range(8):
                for c in range(8):
                    entry = m[max(a, c), min(a, c)]
                    if c <= a:
                        d_ref[d_at(g, k, a, c), :] = entry
                    v_ref[row8(g * 64 + a * 8 + c), :] = -entry

    def scale_block(g, k, j, swap):
        base = pair_base(k, j) if swap else pair_base(j, k)
        for half in range(2):
            rows = range(half * 4, half * 4 + 4)
            acc = {}
            for l in range(8):
                left = {}
                for a in rows:
                    left[a] = w_ref[w_at(g, base + (l * 8 + a if swap else a * 8 + l)), :]
                    c_ref[p_at(g, j, a, l), :] = left[a]
                for c in range(8):
                    right = v_ref[row8(g * 64 + l * 8 + c), :]
                    for a in rows:
                        term = left[a] * right
                        acc[a, c] = term if l == 0 else acc[a, c] + term
            for a in rows:
                for c in range(8):
                    b_ref[p_at(g, j, a, c), :] = acc[a, c]
        for a in range(8):
            for c in range(8):
                w_ref[w_at(g, base + (c * 8 + a if swap else a * 8 + c)), :] = b_ref[p_at(g, j, a, c), :]

    def scale_border(g, k):
        old = [w_ref[w_at(g, OFF_BORDER + k * 8 + m), :] for m in range(8)]
        total = w_ref[w_at(g, OFF_LAST), :]
        for c in range(8):
            new = old[0] * v_ref[row8(g * 64 + c), :]
            for l in range(1, 8):
                new = new + old[l] * v_ref[row8(g * 64 + l * 8 + c), :]
            x_ref[x_at(g, 49 + c), :] = new
            w_ref[w_at(g, OFF_BORDER + k * 8 + c), :] = new
            total = total - new * old[c]
        w_ref[w_at(g, OFF_LAST), :] = total

    def update_pair(g, i, j):
        base = pair_base(i, j)
        for half in range(2):
            rows = range(half * 4, half * 4 + 4)
            acc = {(a, c): w_ref[w_at(g, base + a * 8 + c), :] for a in rows for c in range(8)}
            for m in range(8):
                left = {a: b_ref[p_at(g, i, a, m), :] for a in rows}
                for c in range(8):
                    right = c_ref[p_at(g, j, c, m), :]
                    for a in rows:
                        acc[a, c] = acc[a, c] - left[a] * right
            for a in rows:
                for c in range(8):
                    w_ref[w_at(g, base + a * 8 + c), :] = acc[a, c]

    def update_diag(g, i):
        for rows in (range(0, 6), range(6, 8)):
            acc = {(a, c): d_ref[d_at(g, i, a, c), :] for a in rows for c in range(a + 1)}
            if rows[0]:
                edge = [w_ref[w_at(g, OFF_BORDER + i * 8 + c), :] for c in range(8)]
            for m in range(8):
                left = {a: b_ref[p_at(g, i, a, m), :] for a in rows}
                if rows[0]:
                    last = x_ref[x_at(g, 49 + m), :]
                for c in range(rows[-1] + 1):
                    right = c_ref[p_at(g, i, c, m), :]
                    for a in rows:
                        if c <= a:
                            acc[a, c] = acc[a, c] - left[a] * right
                    if rows[0]:
                        edge[c] = edge[c] - last * right
            for a, c in acc:
                d_ref[d_at(g, i, a, c), :] = acc[a, c]
            if rows[0]:
                for c in range(8):
                    w_ref[w_at(g, OFF_BORDER + i * 8 + c), :] = edge[c]

    def sweep(k, _):
        pivot_block(k)

        def scale_group(g, _):
            lax.fori_loop(0, k, lambda j, z: (scale_block(g, k, j, True), z)[1], 0)
            lax.fori_loop(k + 1, NBLK, lambda j, z: (scale_block(g, k, j, False), z)[1], 0)
            scale_border(g, k)
            return 0

        lax.fori_loop(0, 2, scale_group, 0)

        def update_group(g, _):
            def update_row(t, _):
                i = t + (t >= k).astype(jnp.int32)

                def update_one(s, _):
                    update_pair(g, i, s + (s >= k).astype(jnp.int32))
                    return 0

                lax.fori_loop(0, t, update_one, 0)
                update_diag(g, i)
                return 0

            lax.fori_loop(0, NBLK - 1, update_row, 0)
            return 0

        lax.fori_loop(0, 2, update_group, 0)
        return 0

    lax.fori_loop(0, NBLK, sweep, 0)

    zero = jnp.zeros((8, 128), jnp.float32)
    constant = 0.5 * R * math.log(2.0 * math.pi)

    def finish(g, _):
        w_ref[w_at(g, OFF_LAST), :] = 0.5 * w_ref[w_at(g, OFF_LAST), :]
        for n in range(1, 8):
            w_ref[w_at(g, OFF_LAST + n), :] = zero

        def finish_diag(i, _):
            for d in range(5):
                weight = 1.0 if 0 < d < 4 else 0.5
                for c in range(8):
                    a = (c + d) % 8
                    entry = d_ref[d_at(g, i, max(a, c), min(a, c)), :]
                    w_ref[w_at(g, OFF_DIAG + i * 40 + d * 8 + c), :] = weight * entry
            return 0

        lax.fori_loop(0, NBLK, finish_diag, 0)
        bias = jnp.broadcast_to(prior_ref[...], (8, 128)) - 0.5 * x_ref[x_at(g, 48), :] - constant
        coarse = bias.astype(jnp.bfloat16).astype(jnp.float32)
        w_ref[w_at(g, OFF_BIAS), :] = coarse
        w_ref[w_at(g, OFF_BIAS + 1), :] = bias - coarse
        for n in range(OFF_BIAS + 2, FEATS):
            w_ref[w_at(g, n), :] = zero
        return 0

    lax.fori_loop(0, 2, finish, 0)


def build_products(e_ref, hi_ref, lo_ref):
    width = e_ref.shape[1]
    blocks = [e_ref[i * 8 : i * 8 + 8, :] for i in range(NBLK)]

    def row(i):
        return jnp.broadcast_to(e_ref[i : i + 1, :], (8, width))

    groups = []
    for i in range(NBLK):
        for j in range(i):
            groups += [lambda i=i, j=j, a=a: row(i * 8 + a) * blocks[j] for a in range(8)]
    groups += [lambda j=j: row(48) * blocks[j] for j in range(NBLK)]
    groups += [lambda: row(48) * row(48)]
    for i in range(NBLK):
        for d in range(5):
            groups += [lambda i=i, d=d: blocks[i] * (pltpu.roll(blocks[i], 8 - d, 0) if d else blocks[i])]
    groups += [lambda: jnp.ones((8, width), jnp.float32)]
    groups += [lambda: jnp.zeros((8, width), jnp.float32)] * 2
    for n in range(0, len(groups), 2):
        both = jnp.concatenate([groups[n](), groups[n + 1]()], axis=0)
        head = both.astype(jnp.bfloat16)
        rest = (both - head.astype(jnp.float32)).astype(jnp.bfloat16)
        hi_ref[n * 8 : n * 8 + 16, :] = head
        lo_ref[n * 8 : n * 8 + 16, :] = rest


def score_kernel(
    e_ref, covar_ref, se2_ref, prior_ref, scores_ref, max_ref, sum_ref,
    w_ref, d_ref, b_ref, c_ref, v_ref, x_ref, hi_ref, lo_ref, left_ref,
):
    t = pl.program_id(0)

    @pl.when(t == 0)
    def _():
        invert_all(covar_ref, se2_ref, prior_ref, w_ref, d_ref, b_ref, c_ref, v_ref, x_ref)

    first = (t // 8) * (FEATS * 8) + t % 8
    for n in range(FEATS // 128):
        part = w_ref[pl.ds(first + n * 1024, 128, stride=8), :].T
        head = part.astype(jnp.bfloat16)
        left_ref[0:128, n * 128 : (n + 1) * 128] = head
        left_ref[128:256, n * 128 : (n + 1) * 128] = (part - head.astype(jnp.float32)).astype(jnp.bfloat16)
    build_products(e_ref, hi_ref, lo_ref)
    main = jnp.dot(left_ref[...], hi_ref[...], preferred_element_type=jnp.float32)
    rest = jnp.dot(left_ref[0:128, :], lo_ref[...], preferred_element_type=jnp.float32)
    scores = main[0:128] + (main[128:256] + rest)
    top = jnp.max(scores, axis=0, keepdims=True)
    scores_ref[...] = scores
    max_ref[0] = top
    sum_ref[0] = jnp.sum(jnp.exp(scores - top), axis=0, keepdims=True)


def finish_kernel(scores_ref, stats_ref, other_ref, resp_ref, loglik_ref, mass_ref):
    t = pl.program_id(0)
    m0, m1 = stats_ref[0:1, :], other_ref[0:1, :]
    top = jnp.maximum(m0, m1)
    total = stats_ref[1:2, :] * jnp.exp(m0 - top) + other_ref[1:2, :] * jnp.exp(m1 - top)
    loglik = top + jnp.log(total)
    loglik_ref[...] = loglik
    resp = jnp.exp(scores_ref[...] - loglik)
    resp_ref[...] = resp

    @pl.when(t == 0)
    def _():
        mass_ref[...] = jnp.zeros_like(mass_ref)

    part = resp[:, 0:128]
    for n in range(1, resp.shape[1] // 128):
        part = part + resp[:, n * 128 : (n + 1) * 128]
    mass_ref[...] = mass_ref[...] + part


def score_stage(effects, se_table, se_index, base_root, grid_scale, comp_base, comp_grid, weights):
    pairs = effects.shape[1]
    comps = comp_base.shape[0]
    tiles = pairs // TILE
    covariances = jnp.einsum("uij,ukj->iku", base_root, base_root, precision=HIGHEST)
    pick = (jnp.arange(base_root.shape[0], dtype=jnp.int32)[:, None] == comp_base[None]).astype(jnp.float32)
    scale = grid_scale[comp_grid]
    covar = jnp.einsum("iku,uc->ikc", covariances, pick, precision=HIGHEST) * (scale * scale)
    tile_se = se_table[se_index]
    se2 = jnp.broadcast_to((tile_se * tile_se).T[:, :, None], (R, tiles, comps))
    prior = jnp.log(weights)[None, :]

    whole = lambda shape: pl.BlockSpec(shape, lambda t: (0,) * len(shape))
    return pl.pallas_call(
        score_kernel,
        grid=(tiles,),
        in_specs=[
            pl.BlockSpec((R, TILE), lambda t: (0, t)),
            whole((R, R, comps)),
            whole((R, tiles, comps)),
            whole((1, comps)),
        ],
        out_specs=[
            pl.BlockSpec((comps, TILE), lambda t: (0, t)),
            pl.BlockSpec((1, 1, TILE), lambda t: (t, 0, 0)),
            pl.BlockSpec((1, 1, TILE), lambda t: (t, 0, 0)),
        ],
        out_shape=[
            jax.ShapeDtypeStruct((comps, pairs), jnp.float32),
            jax.ShapeDtypeStruct((tiles, 1, TILE), jnp.float32),
            jax.ShapeDtypeStruct((tiles, 1, TILE), jnp.float32),
        ],
        scratch_shapes=[
            pltpu.VMEM((2 * FEATS * 8, 128), jnp.float32),
            pltpu.VMEM((2 * NBLK * 64 * 8, 128), jnp.float32),
            pltpu.VMEM((2 * NBLK * 64 * 8, 128), jnp.float32),
            pltpu.VMEM((2 * NBLK * 64 * 8, 128), jnp.float32),
            pltpu.VMEM((2 * 64 * 8, 128), jnp.float32),
            pltpu.VMEM((2 * 72 * 8, 128), jnp.float32),
            pltpu.VMEM((FEATS, TILE), jnp.bfloat16),
            pltpu.VMEM((FEATS, TILE), jnp.bfloat16),
            pltpu.VMEM((256, FEATS), jnp.bfloat16),
        ],
        name="scores",
    )(effects, covar, se2, prior)


def per_device(effects, se_table, se_index, base_root, grid_scale, comp_base, comp_grid, weights):
    pairs = effects.shape[1]
    comps = comp_base.shape[0]
    scores, top, total = score_stage(
        effects, se_table, se_index, base_root, grid_scale, comp_base, comp_grid, weights
    )
    stats = jnp.stack([top.reshape(pairs), total.reshape(pairs)])
    other = lax.ppermute(stats, "comp", [(0, 1), (1, 0)])
    block = 2048
    resp, loglik, mass = pl.pallas_call(
        finish_kernel,
        grid=(pairs // block,),
        in_specs=[
            pl.BlockSpec((comps, block), lambda t: (0, t)),
            pl.BlockSpec((2, block), lambda t: (0, t)),
            pl.BlockSpec((2, block), lambda t: (0, t)),
        ],
        out_specs=[
            pl.BlockSpec((comps, block), lambda t: (0, t)),
            pl.BlockSpec((1, block), lambda t: (0, t)),
            pl.BlockSpec((comps, 128), lambda t: (0, 0)),
        ],
        out_shape=[
            jax.ShapeDtypeStruct((comps, pairs), jnp.float32),
            jax.ShapeDtypeStruct((1, pairs), jnp.float32),
            jax.ShapeDtypeStruct((comps, 128), jnp.float32),
        ],
        name="finish",
    )(scores, stats, other)
    local = jnp.sum(mass, axis=1)
    count = lax.axis_size("pairs")
    sent = lax.all_to_all(jnp.broadcast_to(local[None], (count, comps)), "pairs", 0, 0, tiled=True)
    masses = jnp.sum(sent, axis=0)
    log_weights = jnp.log((masses + 1.0) / (pairs * count + comps * lax.axis_size("comp")))
    return (resp, log_weights, loglik.reshape(pairs))


def solution(mesh):
    placed = (P(None, "pairs"), P(), P("pairs"), P(), P(), P("comp"), P("comp"), P("comp"))
    return jax.shard_map(
        per_device,
        mesh=mesh,
        in_specs=placed,
        out_specs=(P("comp", "pairs"), P("comp"), P("pairs")),
        check_vma=False,
    )
```

time: 877 us -> 108 us (0.12)
  other arithmetic: 209 us -> 13 us
  blocking collectives: 214 us -> 20.9 us
  matrix products: 187 us -> 4.61 us
  local copies, waits for them, and re-layouts: 160 us -> 5.63 us
  Pallas kernels: 0 us -> 60.5 us
  waiting for transfers between devices: 57.9 us -> 1.24 us
  loops' own time: 31.8 us -> 0 us
  between operations: 15 us -> 0.74 us
    unnamed x1 -> x0, blocking collectives: 190 us -> none
    another operation x7 -> x1, other arithmetic: 184 us -> 0.84 us  [per_device(): stats = jnp.stack([top.reshape(pairs), total.reshape(pairs)])]
    dot_general x22 -> x2, matrix products: 185 us -> 4.61 us  [the longest x1 2.41 us: score_stage(): jnp.einsum('iku,uc->ikc', covariances, pick, precision=HIGHEST)]
    dynamic_slice x48 -> x0, local copies, waits for them, and re-layouts: 85.4 us -> none  [the longest x32 76.1 us: one_tile(): lax.dynamic_index_in_dim(whiten_table, block_id, 0, keepdims=False)]
    reshape x5 -> x0, local copies, waits for them, and re-layouts: 63.1 us -> none  [the longest x1 39.8 us: per_device(): inverse.reshape(block_count, comp_count, tissues, tissues)]
    pallas_call x0 -> x2, Pallas kernels: none -> 60.5 us  [the longest x1 55.5 us: score_stage(): pl.pallas_call(score_kernel, grid=(tiles,), in_specs=[pl.BlockSpec((R, TI...]
    all_gather x1 -> x0, waiting for transfers between devices: 57.9 us -> none  [per_device(): lax.all_gather(own_inverse, 'pairs', axis=0, tiled=True)]
    another operation x1 -> x0, loops' own time: 31.8 us -> none  [per_device(): lax.fori_loop(0, local_pairs // TILE, one_tile, jnp.zeros((comp_count, lo...]
where the time goes in v1:
time: 108 us; the launch traced here: 107 us
  Pallas kernels  60.5 us (56%)
  blocking collectives  20.9 us (19%)
  other arithmetic  13 us (12%)
  local copies, waits for them, and re-layouts  5.63 us (5%)
  matrix products  4.61 us (4%)
  waiting for transfers between devices  1.24 us (1%)
    pallas_call x1, Pallas kernels, score_stage(): pl.pallas_call(score_kernel, grid=(tiles,), in_specs=[pl.BlockSpec((R, TI...  55.5 us
    all_to_all x1, blocking collectives, per_device(): lax.all_to_all(jnp.broadcast_to(local[None], (count, comps)), 'pairs', 0,...  20.9 us
    mul x1, other arithmetic, score_stage(): scale * scale  9.98 us
    pallas_call x1, Pallas kernels, per_device(): pl.pallas_call(finish_kernel, grid=(pairs // block,), in_specs=[pl.BlockS...  4.96 us
    dot_general x1, matrix products, score_stage(): jnp.einsum('iku,uc->ikc', covariances, pick, precision=HIGHEST)  2.41 us
    dot_general x1, matrix products, score_stage(): jnp.einsum('uij,ukj->iku', base_root, base_root, precision=HIGHEST)  2.19 us
  transfers between devices with their start and end apart: 1, of which 1 were waited for; matrix products, arithmetic and copies ran while one was open for 0% of the time, Pallas kernels for 0%

profile of v1, /device:TPU:0, one launch (start us, length us, event | category | flops | bytes accessed | tf_op | source)
XLA Modules:
  0.0 106.7 jit_solution(3940041600855816494)
XLA Ops:
  0.6 0.0 copy-start
  0.6 0.0 copy-start.4
  0.7 0.0 copy-start.3
  0.7 0.7 compare_select_fusion
  1.3 1.2 %log_bitcast_fusion.prior_ref = f32[1,128]{1,0:T(1,128)} fusion(f32[128]{0:T(128)} %param.15), kind=kLoop, calls=%fused_computation.29 | loop fusion | bytes 1024 | tf_op jit(solution)/shard_map/broadcast_in_dim | solution.py:320
  2.5 0.0 copy-done
  2.5 0.6 gather_fusion
  3.1 1.9 %fusion.5 = (f32[1]{0:T(128)}, f32[1]{0:T(128)}, f32[1]{0:T(128)}, f32[1]{0:T(128)}, f32[1]{0:T(128)}, /*index=5*/f32[1]{0:T(128)}, f32[1]{0:T(128)}, f32[1]{0:T...) fusion(f32[16]{0:T(128)} %param.12), kind=kLoop, calls=%fused_computation.30 | loop fusion | bytes 128 | tf_op jit(solution)/shard_map/gather | solution.py:316
  5.0 0.1 copy.16
  5.1 2.2 %convolution_bitcast_fusion = f32[49,49,16]{0,1,2:T(8,128)S(1)} fusion(f32[16,49,49]{2,0,1:T(8,128)} %param.11), kind=kOutput, calls=%fused_computation.2 | convolution fusion | flops 22588608 | bytes 307328 | tf_op jit(solution)/shard_map/uij,ukj->iku/dot_general | solution.py:314
  7.3 0.3 copy.15
  7.6 0.0 copy-done.4
  7.6 10.0 %fusion.4 = f32[128]{0:T(128)S(1)} fusion(s32[128]{0:T(128)S(1)} %copy-done.4, f32[]{:T(128)} %bitcast.2, f32[]{:T(128)} %bitcast.3, f32[]{:T(128)} %bitcast.4, f32[]{:T(128)} %bitcast.5, f32[]{:T(128)} %bitcast.6, f32[]{:T(128)} %bitcast.7, f32[]{:T(128)} %bitcast.8, f32[]{:T(128)} %bitcast.9, f32[]{:T(128)} %bitcast.10, f32[]{:T(128)} %bitcast.11, ...), kind=kLoop, calls=%fused_computation.27 | loop fusion | flops 4352 | bytes 1088 | tf_op jit(solution)/shard_map/mul | solution.py:317
  17.6 0.0 copy-done.3
  17.6 2.4 %convolution_multiply_fusion.covar_ref = f32[49,49,128]{2,1,0:T(8,128)} fusion(f32[49,49,16]{1,2,0:T(8,128)S(1)} %copy.15, f32[128]{0:T(128)S(1)} %fusion.4, s32[128]{0:T(128)S(1)} %copy-done.3), kind=kOutput, calls=%fused_computation.1 | convolution fusion | flops 59316352 | bytes 1384000 | tf_op jit(solution)/shard_map/iku,uc->ikc/dot_general | solution.py:317
  20.0 0.9 broadcast_in_dim.12.se2_ref
  21.0 55.5 %scores.1 = (f32[128,8192]{1,0:T(8,128)}, f32[16,1,512]{2,1,0:T(1,128)}, f32[16,1,512]{2,1,0:T(1,128)}) custom-call(f32[49,8192]{1,0:T(8,128)} %e_ref.1, f32[49,49,128]{2,1,0:T(8,128)} %convolution_multiply_fusion.covar_ref, f32[49,16,128]{2,1,0:T(8,128)} %broadcast_in_dim.12.se2_ref, f32[1,128]{1,0:T(1,128)} %log_bitcast_fusion.prior_ref), custom_call_target="tpu_custom_call" | custom-call | tf_op jit(solution)/shard_map/scores/pallas_call | solution.py:323
  76.5 0.8 pad_maximum_fusion.stats_ref
  77.3 0.0 copy-start.1
  77.3 0.1 collective-permute-start
  77.4 1.2 %collective-permute-done.other_ref = f32[2,8192]{1,0:T(2,128)S(1)} collective-permute-done((f32[2,8192]{1,0:T(2,128)S(1)}, f32[2,8192]{1,0:T(2,128)S(1)}, u32[]{:S(2)}, u32[]{:S(2)}) %collective-permute-start) | collective-permute-done | bytes 65568 | tf_op jit(solution)/shard_map/ppermute | solution.py:364
  78.7 0.0 copy-start.2
  78.7 0.0 copy-done.1
  78.7 0.6 copy-done.2
  79.3 5.0 %finish.1 = (f32[128,8192]{1,0:T(8,128)}, f32[1,8192]{1,0:T(1,128)}, f32[128,128]{1,0:T(8,128)}) custom-call(f32[128,8192]{1,0:T(8,128)} %get-tuple-element.9.scores_ref, f32[2,8192]{1,0:T(2,128)} %copy-done.1, f32[2,8192]{1,0:T(2,128)} %copy-done.2), custom_call_target="tpu_custom_call" | custom-call | tf_op jit(solution)/shard_map/finish/pallas_call | solution.py:366
  84.2 0.9 reduce_sum.18
  85.2 20.9 %all_to_all.6 = f32[64,1,128]{2,1,0:T(1,128)S(1)} all-to-all(f32[64,1,128]{2,1,0:T(1,128)S(1)} %broadcast_in_dim.28), channel_id=1, replica_groups=mesh['pairs'=64,'comp'=2] {'pairs'}, dimensions={0} | all-to-all | bytes 65536 | tf_op jit(solution)/shard_map/all_to_all | solution.py:388
  106.2 0.5 multiply_log_fusion
  (4 shorter events, 0.1 us)
Async XLA Ops:
  0.6 1.9 %copy-start = (f32[16,49]{1,0:T(8,128)S(1)}, f32[16,49]{1,0:T(8,128)}, u32[]{:S(2)}) copy-start(f32[16,49]{1,0:T(8,128)} %param.9) | copy-start | bytes 9412
  0.6 7.0 %copy-start.4 = (s32[128]{0:T(128)S(1)}, s32[128]{0:T(128)}, u32[]{:S(2)}) copy-start(s32[128]{0:T(128)} %param.14) | copy-start | bytes 1540
  0.7 17.0 %copy-start.3 = (s32[128]{0:T(128)S(1)}, s32[128]{0:T(128)}, u32[]{:S(2)}) copy-start(s32[128]{0:T(128)} %param.13) | copy-start | bytes 1540
  77.3 1.3 %copy-start.1 = (f32[2,8192]{1,0:T(2,128)}, f32[2,8192]{1,0:T(2,128)S(1)}, u32[]{:S(2)}) copy-start(f32[2,8192]{1,0:T(2,128)S(1)} %pad_maximum_fusion.stats_ref) | copy-start | bytes 196612
  77.3 1.3 %collective-permute-start = (f32[2,8192]{1,0:T(2,128)S(1)}, f32[2,8192]{1,0:T(2,128)S(1)}, u32[]{:S(2)}, u32[]{:S(2)}) collective-permute-start(f32[2,8192]{1,0:T(2,128)S(1)} %pad_maximum_fusion.stats_ref), channel_id=1, source_target_pairs={{0,1},{1,0},{2,3},{3,2},{4,5},{5,4},{6,7},{7,6},{8,9},{9,8},{10,11... | collective-permute-start | bytes 196616 | tf_op jit(solution)/shard_map/ppermute | solution.py:364
  78.7 0.6 copy-start.2

commit v2 on v1

--- a/solution.py
+++ b/solution.py
@@ -1,3 +1,4 @@
+import functools
 import math
 
 import jax
@@ -22,7 +23,7 @@
     return pl.ds(pl.multiple_of(index * 8, 8), 8)
 
 
-def invert_all(covar_ref, se2_ref, prior_ref, w_ref, d_ref, b_ref, c_ref, v_ref, x_ref):
+def invert_all(covar_ref, se2_ref, weight_ref, w_ref, d_ref, b_ref, c_ref, v_ref, x_ref):
     def w_at(g, f):
         return row8(g * FEATS + f)
 
@@ -224,7 +225,7 @@
             return 0
 
         lax.fori_loop(0, NBLK, finish_diag, 0)
-        bias = jnp.broadcast_to(prior_ref[...], (8, 128)) - 0.5 * x_ref[x_at(g, 48), :] - constant
+        bias = jnp.broadcast_to(jnp.log(weight_ref[...]), (8, 128)) - 0.5 * x_ref[x_at(g, 48), :] - constant
         coarse = bias.astype(jnp.bfloat16).astype(jnp.float32)
         w_ref[w_at(g, OFF_BIAS), :] = coarse
         w_ref[w_at(g, OFF_BIAS + 1), :] = bias - coarse
@@ -261,15 +262,49 @@
         lo_ref[n * 8 : n * 8 + 16, :] = rest
 
 
+def prepare(se_ref, index_ref, root_ref, grid_ref, base_ref, level_ref, covar_ref, se2_ref, cov_ref, rows_ref):
+    units = root_ref.shape[0]
+    for u in range(units):
+        root = root_ref[u]
+        cov_ref[u * 56 : u * 56 + R, 0:R] = lax.dot_general(
+            root, root, (((1,), (1,)), ((), ())), precision=HIGHEST, preferred_element_type=jnp.float32
+        )
+    comps = base_ref.shape[1]
+    pick = (lax.broadcasted_iota(jnp.int32, (units, comps), 0) == base_ref[...]).astype(jnp.bfloat16)
+    scale = jnp.zeros((1, comps), jnp.float32)
+    for n in range(grid_ref.shape[0]):
+        scale = jnp.where(level_ref[...] == n, grid_ref[n], scale)
+    scale2 = scale * scale
+
+    def one_row(i, _):
+        part = cov_ref[pl.ds(i, units, stride=56), :].T[0:56]
+        total = None
+        for _ in range(3):
+            head = part.astype(jnp.bfloat16)
+            term = jnp.dot(head, pick, preferred_element_type=jnp.float32)
+            total = term if total is None else total + term
+            part = part - head.astype(jnp.float32)
+        covar_ref[i] = total * scale2
+        return 0
+
+    lax.fori_loop(0, R, one_row, 0, unroll=7)
+    for t in range(index_ref.shape[0]):
+        rows_ref[t : t + 1, 0:R] = se_ref[pl.ds(index_ref[t], 1), :]
+    squares = rows_ref[...] * rows_ref[...]
+    for i in range(R):
+        se2_ref[i] = jnp.broadcast_to(squares[:, i : i + 1], se2_ref.shape[1:])
+
+
 def score_kernel(
-    e_ref, covar_ref, se2_ref, prior_ref, scores_ref, max_ref, sum_ref,
-    w_ref, d_ref, b_ref, c_ref, v_ref, x_ref, hi_ref, lo_ref, left_ref,
+    e_ref, se_ref, index_ref, root_ref, grid_ref, base_ref, level_ref, weight_ref, scores_ref, stats_ref,
+    covar_ref, se2_ref, cov_ref, rows_ref, w_ref, d_ref, b_ref, c_ref, v_ref, x_ref, hi_ref, lo_ref, left_ref,
 ):
     t = pl.program_id(0)
 
     @pl.when(t == 0)
     def _():
-        invert_all(covar_ref, se2_ref, prior_ref, w_ref, d_ref, b_ref, c_ref, v_ref, x_ref)
+        prepare(se_ref, index_ref, root_ref, grid_ref, base_ref, level_ref, covar_ref, se2_ref, cov_ref, rows_ref)
+        invert_all(covar_ref, se2_ref, weight_ref, w_ref, d_ref, b_ref, c_ref, v_ref, x_ref)
 
     first = (t // 8) * (FEATS * 8) + t % 8
     for n in range(FEATS // 128):
@@ -282,64 +317,101 @@
     rest = jnp.dot(left_ref[0:128, :], lo_ref[...], preferred_element_type=jnp.float32)
     scores = main[0:128] + (main[128:256] + rest)
     top = jnp.max(scores, axis=0, keepdims=True)
-    scores_ref[...] = scores
-    max_ref[0] = top
-    sum_ref[0] = jnp.sum(jnp.exp(scores - top), axis=0, keepdims=True)
-
-
-def finish_kernel(scores_ref, stats_ref, other_ref, resp_ref, loglik_ref, mass_ref):
-    t = pl.program_id(0)
-    m0, m1 = stats_ref[0:1, :], other_ref[0:1, :]
-    top = jnp.maximum(m0, m1)
-    total = stats_ref[1:2, :] * jnp.exp(m0 - top) + other_ref[1:2, :] * jnp.exp(m1 - top)
-    loglik = top + jnp.log(total)
-    loglik_ref[...] = loglik
-    resp = jnp.exp(scores_ref[...] - loglik)
-    resp_ref[...] = resp
-
-    @pl.when(t == 0)
-    def _():
-        mass_ref[...] = jnp.zeros_like(mass_ref)
-
-    part = resp[:, 0:128]
-    for n in range(1, resp.shape[1] // 128):
-        part = part + resp[:, n * 128 : (n + 1) * 128]
-    mass_ref[...] = mass_ref[...] + part
+    scores_ref[:, pl.ds(pl.multiple_of(t * TILE, TILE), TILE)] = scores
+    stats_ref[0:1, :] = top
+    stats_ref[1:2, :] = jnp.sum(jnp.exp(scores - top), axis=0, keepdims=True)
+
+
+def tail_kernel(
+    count, all_pairs, all_comps, scores_ref, stats_ref, resp_ref, loglik_ref, logw_ref,
+    other_ref, mine_ref, slots_ref, pair_sems, send_sems, recv_sems,
+):
+    chip, core = lax.axis_index("pairs"), lax.axis_index("comp")
+    mesh_id = pl.DeviceIdType.MESH
+    barrier = pltpu.get_barrier_semaphore()
+    pl.semaphore_signal(barrier, inc=1, device_id=(chip, 1 - core), device_id_type=mesh_id)
+
+    def greet(d, _):
+        pl.semaphore_signal(barrier, inc=1, device_id=((chip + d) % count, core), device_id_type=mesh_id)
+        return 0
+
+    lax.fori_loop(1, count, greet, 0)
+    pl.semaphore_wait(barrier, count)
+    swap = pltpu.make_async_remote_copy(
+        src_ref=stats_ref, dst_ref=other_ref, send_sem=pair_sems.at[0], recv_sem=pair_sems.at[1],
+        device_id=(chip, 1 - core), device_id_type=mesh_id,
+    )
+    swap.start()
+    swap.wait()
+
+    def one_part(n, mass):
+        cols = pl.ds(pl.multiple_of(n * TILE, TILE), TILE)
+        m0, m1 = stats_ref[0:1, cols], other_ref[0:1, cols]
+        top = jnp.maximum(m0, m1)
+        total = stats_ref[1:2, cols] * jnp.exp(m0 - top) + other_ref[1:2, cols] * jnp.exp(m1 - top)
+        loglik = top + jnp.log(total)
+        loglik_ref[0:1, cols] = loglik
+        resp = jnp.exp(scores_ref[:, cols] - loglik)
+        resp_ref[:, cols] = resp
+        for j in range(TILE // 128):
+            mass = mass + resp[:, j * 128 : (j + 1) * 128]
+        return mass
+
+    mass = lax.fori_loop(0, scores_ref.shape[1] // TILE, one_part, jnp.zeros((128, 128), jnp.float32))
+    own = jnp.sum(mass.T, axis=0, keepdims=True)
+    mine_ref[...] = own
+    slots_ref[chip] = own
+
+    def copy_to(peer, slot):
+        return pltpu.make_async_remote_copy(
+            src_ref=mine_ref, dst_ref=slots_ref.at[slot], send_sem=send_sems.at[peer], recv_sem=recv_sems.at[slot],
+            device_id=(peer, core), device_id_type=mesh_id,
+        )
+
+    def send(d, _):
+        copy_to((chip + d) % count, chip).start()
+        return 0
+
+    lax.fori_loop(1, count, send, 0)
+
+    def receive(d, _):
+        peer = (chip + d) % count
+        copy_to(peer, peer).wait_recv()
+        return 0
+
+    lax.fori_loop(1, count, receive, 0)
+    masses = slots_ref[0]
+    for n in range(1, count):
+        masses = masses + slots_ref[n]
+    logw_ref[...] = jnp.log((masses + 1.0) / (all_pairs + all_comps))
+
+    def sent(d, _):
+        copy_to((chip + d) % count, chip).wait_send()
+        return 0
+
+    lax.fori_loop(1, count, sent, 0)
 
 
 def score_stage(effects, se_table, se_index, base_root, grid_scale, comp_base, comp_grid, weights):
     pairs = effects.shape[1]
     comps = comp_base.shape[0]
     tiles = pairs // TILE
-    covariances = jnp.einsum("uij,ukj->iku", base_root, base_root, precision=HIGHEST)
-    pick = (jnp.arange(base_root.shape[0], dtype=jnp.int32)[:, None] == comp_base[None]).astype(jnp.float32)
-    scale = grid_scale[comp_grid]
-    covar = jnp.einsum("iku,uc->ikc", covariances, pick, precision=HIGHEST) * (scale * scale)
-    tile_se = se_table[se_index]
-    se2 = jnp.broadcast_to((tile_se * tile_se).T[:, :, None], (R, tiles, comps))
-    prior = jnp.log(weights)[None, :]
-
-    whole = lambda shape: pl.BlockSpec(shape, lambda t: (0,) * len(shape))
+    vmem = pl.BlockSpec(memory_space=pltpu.VMEM)
+    smem = pl.BlockSpec(memory_space=pltpu.SMEM)
     return pl.pallas_call(
         score_kernel,
         grid=(tiles,),
-        in_specs=[
-            pl.BlockSpec((R, TILE), lambda t: (0, t)),
-            whole((R, R, comps)),
-            whole((R, tiles, comps)),
-            whole((1, comps)),
-        ],
-        out_specs=[
-            pl.BlockSpec((comps, TILE), lambda t: (0, t)),
-            pl.BlockSpec((1, 1, TILE), lambda t: (t, 0, 0)),
-            pl.BlockSpec((1, 1, TILE), lambda t: (t, 0, 0)),
-        ],
+        in_specs=[pl.BlockSpec((R, TILE), lambda t: (0, t)), vmem, smem, vmem, smem, vmem, vmem, vmem],
+        out_specs=[vmem, pl.BlockSpec((2, TILE), lambda t: (0, t))],
         out_shape=[
-            jax.ShapeDtypeStruct((comps, pairs), jnp.float32),
-            jax.ShapeDtypeStruct((tiles, 1, TILE), jnp.float32),
-            jax.ShapeDtypeStruct((tiles, 1, TILE), jnp.float32),
+            pltpu.VMEM((comps, pairs), jnp.float32),
+            jax.ShapeDtypeStruct((2, pairs), jnp.float32),
         ],
         scratch_shapes=[
+            pltpu.VMEM((R, 56, comps), jnp.float32),
+            pltpu.VMEM((R, tiles, comps), jnp.float32),
+            pltpu.VMEM((base_root.shape[0] * 56, 128), jnp.float32),
+            pltpu.VMEM((tiles, 128), jnp.float32),
             pltpu.VMEM((2 * FEATS * 8, 128), jnp.float32),
             pltpu.VMEM((2 * NBLK * 64 * 8, 128), jnp.float32),
             pltpu.VMEM((2 * NBLK * 64 * 8, 128), jnp.float32),
@@ -350,45 +422,45 @@
             pltpu.VMEM((FEATS, TILE), jnp.bfloat16),
             pltpu.VMEM((256, FEATS), jnp.bfloat16),
         ],
+        compiler_params=pltpu.CompilerParams(vmem_limit_bytes=44 * 1024 * 1024),
         name="scores",
-    )(effects, covar, se2, prior)
+    )(
+        effects, se_table, se_index, base_root, grid_scale,
+        comp_base.reshape(1, comps), comp_grid.reshape(1, comps), weights.reshape(1, comps),
+    )
 
 
 def per_device(effects, se_table, se_index, base_root, grid_scale, comp_base, comp_grid, weights):
     pairs = effects.shape[1]
     comps = comp_base.shape[0]
-    scores, top, total = score_stage(
+    scores, stats = score_stage(
         effects, se_table, se_index, base_root, grid_scale, comp_base, comp_grid, weights
     )
-    stats = jnp.stack([top.reshape(pairs), total.reshape(pairs)])
-    other = lax.ppermute(stats, "comp", [(0, 1), (1, 0)])
-    block = 2048
-    resp, loglik, mass = pl.pallas_call(
-        finish_kernel,
-        grid=(pairs // block,),
-        in_specs=[
-            pl.BlockSpec((comps, block), lambda t: (0, t)),
-            pl.BlockSpec((2, block), lambda t: (0, t)),
-            pl.BlockSpec((2, block), lambda t: (0, t)),
+    count = lax.axis_size("pairs")
+    vmem = pl.BlockSpec(memory_space=pltpu.VMEM)
+    resp, loglik, logw = pl.pallas_call(
+        functools.partial(tail_kernel, count, pairs * count, comps * lax.axis_size("comp")),
+        in_specs=[vmem, vmem],
+        out_specs=[vmem, vmem, vmem],
+        out_shape=[
+            pltpu.VMEM((comps, pairs), jnp.float32),
+            jax.ShapeDtypeStruct((1, pairs), jnp.float32),
+            jax.ShapeDtypeStruct((1, comps), jnp.float32),
         ],
-        out_specs=[
-            pl.BlockSpec((comps, block), lambda t: (0, t)),
-            pl.BlockSpec((1, block), lambda t: (0, t)),
-            pl.BlockSpec((comps, 128), lambda t: (0, 0)),
+        scratch_shapes=[
+            pltpu.VMEM((2, pairs), jnp.float32),
+            pltpu.VMEM((1, comps), jnp.float32),
+            pltpu.VMEM((count, 1, comps), jnp.float32),
+            pltpu.SemaphoreType.DMA((2,)),
+            pltpu.SemaphoreType.DMA((count,)),
+            pltpu.SemaphoreType.DMA((count,)),
         ],
-        out_shape=[
-            jax.ShapeDtypeStruct((comps, pairs), jnp.float32),
-            jax.ShapeDtypeStruct((1, pairs), jnp.float32),
-            jax.ShapeDtypeStruct((comps, 128), jnp.float32),
-        ],
-        name="finish",
-    )(scores, stats, other)
-    local = jnp.sum(mass, axis=1)
-    count = lax.axis_size("pairs")
-    sent = lax.all_to_all(jnp.broadcast_to(local[None], (count, comps)), "pairs", 0, 0, tiled=True)
-    masses = jnp.sum(sent, axis=0)
-    log_weights = jnp.log((masses + 1.0) / (pairs * count + comps * lax.axis_size("comp")))
-    return (resp, log_weights, loglik.reshape(pairs))
+        compiler_params=pltpu.CompilerParams(
+            collective_id=0, has_side_effects=True, vmem_limit_bytes=24 * 1024 * 1024
+        ),
+        name="tail",
+    )(scores, stats)
+    return (resp, logw.reshape(comps), loglik.reshape(pairs))
 
 
 def solution(mesh):

time: 108 us -> 87.2 us (0.81)
  blocking collectives: 20.9 us -> 0 us
  Pallas kernels: 60.5 us -> 76.2 us
  other arithmetic: 13 us -> 0 us
  matrix products: 4.61 us -> 0 us
  local copies, waits for them, and re-layouts: 5.63 us -> 9.74 us
  waiting for transfers between devices: 1.24 us -> 0 us
    all_to_all x1 -> x0, blocking collectives: 20.9 us -> none  [per_device(): lax.all_to_all(jnp.broadcast_to(local[None], (count, comps)), 'pairs', 0,...]
    pallas_call x1, Pallas kernels: 4.96 us -> 18.9 us  [per_device(): pl.pallas_call(functools.partial(tail_kernel, count, pairs * count, comps...]
    mul x2 -> x0, other arithmetic: 9.98 us -> none  [the longest x1 9.98 us: score_stage(): scale * scale]
    unnamed x10 -> x18, local copies, waits for them, and re-layouts: 0.64 us -> 9.74 us
    dot_general x2 -> x0, matrix products: 4.61 us -> none  [the longest x1 2.41 us: score_stage(): jnp.einsum('iku,uc->ikc', covariances, pick, precision=HIGHEST)]
    gather x2 -> x0, local copies, waits for them, and re-layouts: 2.51 us -> none  [the longest x1 1.95 us: score_stage(): scale = grid_scale[comp_grid]]
    broadcast_in_dim x3 -> x0, local copies, waits for them, and re-layouts: 2.11 us -> none  [the longest x1 1.17 us: score_stage(): prior = jnp.log(weights)[None, :]]
    pallas_call x1, Pallas kernels: 55.5 us -> 57.3 us  [score_stage(): pl.pallas_call(score_kernel, grid=(tiles,), in_specs=[pl.BlockSpec((R, TI...]
  transfers between devices with their start and end apart: 1 -> 0, of which waited for: 1 -> 0; matrix products, arithmetic and copies ran while one was open for 0% -> 0% of each run, Pallas kernels for 0% -> 0%
where the time goes in v2:
time: 87.2 us; the launch traced here: 86.6 us
  Pallas kernels  76.2 us (87%)
  local copies, waits for them, and re-layouts  9.74 us (11%)
    pallas_call x1, Pallas kernels, score_stage(): pl.pallas_call(score_kernel, grid=(tiles,), in_specs=[pl.BlockSpec((R, TI...  57.3 us
    pallas_call x1, Pallas kernels, per_device(): pl.pallas_call(functools.partial(tail_kernel, count, pairs * count, comps...  18.9 us
    unnamed x18, local copies, waits for them, and re-layouts  9.74 us

profile of v2, /device:TPU:0, one launch (start us, length us, event | category | flops | bytes accessed | tf_op | source)
XLA Modules:
  0.0 86.6 jit_solution(13171613845294187255)
XLA Ops:
  0.6 1.1 %copy.11.root_ref = f32[16,49,49]{2,1,0:T(8,128)S(1)} copy(f32[16,49,49]{2,0,1:T(8,128)} %param.11) | data formatting | bytes 307328 | tf_op args[3]
  1.8 0.0 copy-start
  1.8 1.5 %copy-done = f32[49,8192]{1,0:T(8,128)S(1)} copy-done((f32[49,8192]{1,0:T(8,128)S(1)}, f32[49,8192]{1,0:T(8,128)}, u32[]{:S(2)}) %copy-start) | copy-done | bytes 1605656
  3.3 0.0 copy-start.1
  3.3 0.7 copy-done.1
  4.0 0.0 copy-start.2
  4.0 0.7 copy-done.2
  4.6 0.0 copy-start.3
  4.6 0.7 copy-done.3
  5.3 0.0 copy-start.4
  5.3 0.7 copy-done.4
  5.9 0.0 copy-start.5
  5.9 0.7 copy-done.5
  6.6 0.0 copy-start.6
  6.6 0.7 copy-done.6
  7.2 57.3 %scores.1 = (f32[128,8192]{1,0:T(8,128)S(1)}, f32[2,8192]{1,0:T(2,128)S(1)}) custom-call(f32[49,8192]{1,0:T(8,128)S(1)} %copy-done, f32[16,49]{1,0:T(8,128)S(1)} %copy-done.1, s32[16]{0:T(128)S(1)} %copy-done.2, f32[16,49,49]{2,1,0:T(8,128)S(1)} %copy.11.root_ref, f32[16]{0:T(128)S(1)} %copy-done.3, s32[1,128]{1,0:T(1,128)S(1)} %bitcast.6, ...), custom_call_target="tpu_custom_call" | custom-call | tf_op jit(solution)/shard_map/scores/pallas_call | solution.py:401
  64.5 18.9 %tail.1 = (f32[128,8192]{1,0:T(8,128)S(1)}, f32[1,8192]{1,0:T(1,128)S(1)}, f32[1,128]{1,0:T(1,128)S(1)}) custom-call(f32[128,8192]{1,0:T(8,128)S(1)} %get-tuple-element.8.scores_ref, f32[2,8192]{1,0:T(2,128)S(1)} %get-tuple-element.9.stats_ref), custom_call_target="tpu_custom_call" | custom-call | tf_op jit(solution)/shard_map/tail/pallas_call | solution.py:441
  83.4 2.0 %copy.15 = f32[128,8192]{1,0:T(8,128)} copy(f32[128,8192]{1,0:T(8,128)S(1)} %get-tuple-element.13) | data formatting | bytes 8388608
  85.4 0.5 copy.16
  85.9 0.6 copy.17
Async XLA Ops:
  1.8 1.5 %copy-start = (f32[49,8192]{1,0:T(8,128)S(1)}, f32[49,8192]{1,0:T(8,128)}, u32[]{:S(2)}) copy-start(f32[49,8192]{1,0:T(8,128)} %e_ref.1) | copy-start | bytes 4816900
  3.3 0.7 copy-start.1
  4.0 0.7 copy-start.2
  4.6 0.7 copy-start.3
  5.3 0.7 copy-start.4
  5.9 0.7 copy-start.5
  6.6 0.7 copy-start.6

commit v3 on v2

--- a/solution.py
+++ b/solution.py
@@ -263,9 +263,9 @@
 
 
 def prepare(se_ref, index_ref, root_ref, grid_ref, base_ref, level_ref, covar_ref, se2_ref, cov_ref, rows_ref):
-    units = root_ref.shape[0]
+    units = root_ref.shape[1]
     for u in range(units):
-        root = root_ref[u]
+        root = root_ref[:, u, :]
         cov_ref[u * 56 : u * 56 + R, 0:R] = lax.dot_general(
             root, root, (((1,), (1,)), ((), ())), precision=HIGHEST, preferred_element_type=jnp.float32
         )
@@ -295,35 +295,85 @@
         se2_ref[i] = jnp.broadcast_to(squares[:, i : i + 1], se2_ref.shape[1:])
 
 
-def score_kernel(
-    e_ref, se_ref, index_ref, root_ref, grid_ref, base_ref, level_ref, weight_ref, scores_ref, stats_ref,
-    covar_ref, se2_ref, cov_ref, rows_ref, w_ref, d_ref, b_ref, c_ref, v_ref, x_ref, hi_ref, lo_ref, left_ref,
+def sweep_kernel(
+    se_in, index_in, root_in, grid_in, base_in, level_in, weight_in, w_ref,
+    se_ref, index_ref, root_ref, grid_ref, base_ref, level_ref, weight_ref, sems,
+    covar_ref, se2_ref, cov_ref, rows_ref, d_ref, b_ref, c_ref, v_ref, x_ref,
 ):
-    t = pl.program_id(0)
-
-    @pl.when(t == 0)
-    def _():
-        prepare(se_ref, index_ref, root_ref, grid_ref, base_ref, level_ref, covar_ref, se2_ref, cov_ref, rows_ref)
-        invert_all(covar_ref, se2_ref, weight_ref, w_ref, d_ref, b_ref, c_ref, v_ref, x_ref)
-
+    sources = (se_in, index_in, root_in, grid_in, base_in, level_in, weight_in)
+    places = (se_ref, index_ref, root_ref, grid_ref, base_ref, level_ref, weight_ref)
+    copies = [pltpu.make_async_copy(a, b, sems.at[n]) for n, (a, b) in enumerate(zip(sources, places))]
+    for copy in copies:
+        copy.start()
+    for copy in copies:
+        copy.wait()
+    prepare(se_ref, index_ref, root_ref, grid_ref, base_ref, level_ref, covar_ref, se2_ref, cov_ref, rows_ref)
+    invert_all(covar_ref, se2_ref, weight_ref, w_ref, d_ref, b_ref, c_ref, v_ref, x_ref)
+
+
+def sweep_stage(se_table, se_index, base_root, grid_scale, comp_base, comp_grid, weights):
+    tissues = se_table.shape[1]
+    units = base_root.shape[0]
+    tiles = se_index.shape[0]
+    comps = comp_base.shape[0]
+    panel = pltpu.VMEM((2 * NBLK * 64 * 8, 128), jnp.float32)
+    return pl.pallas_call(
+        sweep_kernel,
+        in_specs=[pl.BlockSpec(memory_space=pltpu.HBM)] * 7,
+        out_specs=pl.BlockSpec(memory_space=pltpu.VMEM),
+        out_shape=pltpu.VMEM((2 * FEATS * 8, 128), jnp.float32),
+        scratch_shapes=[
+            pltpu.VMEM(se_table.shape, jnp.float32),
+            pltpu.SMEM((tiles,), jnp.int32),
+            pltpu.VMEM((tissues, units, tissues), jnp.float32),
+            pltpu.SMEM(grid_scale.shape, jnp.float32),
+            pltpu.VMEM((1, comps), jnp.int32),
+            pltpu.VMEM((1, comps), jnp.int32),
+            pltpu.VMEM((1, comps), jnp.float32),
+            pltpu.SemaphoreType.DMA((7,)),
+            pltpu.VMEM((R, 56, comps), jnp.float32),
+            pltpu.VMEM((R, tiles, comps), jnp.float32),
+            pltpu.VMEM((units * 56, 128), jnp.float32),
+            pltpu.VMEM((tiles, 128), jnp.float32),
+            panel,
+            panel,
+            panel,
+            pltpu.VMEM((2 * 64 * 8, 128), jnp.float32),
+            pltpu.VMEM((2 * 72 * 8, 128), jnp.float32),
+        ],
+        compiler_params=pltpu.CompilerParams(vmem_limit_bytes=32 * 1024 * 1024),
+        cost_estimate=pl.CostEstimate(flops=250_000_000, bytes_accessed=60_000_000, transcendentals=0),
+        name="sweep",
+    )(
+        se_table, se_index, base_root.transpose(1, 0, 2), grid_scale,
+        comp_base.reshape(1, comps), comp_grid.reshape(1, comps), weights.reshape(1, comps),
+    )
+
+
+def build_tile(t, e_ref, w_ref, hi_ref, lo_ref, left_ref):
     first = (t // 8) * (FEATS * 8) + t % 8
     for n in range(FEATS // 128):
         part = w_ref[pl.ds(first + n * 1024, 128, stride=8), :].T
         head = part.astype(jnp.bfloat16)
         left_ref[0:128, n * 128 : (n + 1) * 128] = head
         left_ref[128:256, n * 128 : (n + 1) * 128] = (part - head.astype(jnp.float32)).astype(jnp.bfloat16)
-    build_products(e_ref, hi_ref, lo_ref)
+    build_products(e_ref.at[:, pl.ds(pl.multiple_of(t * TILE, TILE), TILE)], hi_ref, lo_ref)
+
+
+def score_tile(t, hi_ref, lo_ref, left_ref, scores_ref, stats_ref):
+    cols = pl.ds(pl.multiple_of(t * TILE, TILE), TILE)
     main = jnp.dot(left_ref[...], hi_ref[...], preferred_element_type=jnp.float32)
     rest = jnp.dot(left_ref[0:128, :], lo_ref[...], preferred_element_type=jnp.float32)
     scores = main[0:128] + (main[128:256] + rest)
     top = jnp.max(scores, axis=0, keepdims=True)
-    scores_ref[:, pl.ds(pl.multiple_of(t * TILE, TILE), TILE)] = scores
-    stats_ref[0:1, :] = top
-    stats_ref[1:2, :] = jnp.sum(jnp.exp(scores - top), axis=0, keepdims=True)
-
-
-def tail_kernel(
-    count, all_pairs, all_comps, scores_ref, stats_ref, resp_ref, loglik_ref, logw_ref,
+    scores_ref[:, cols] = scores
+    stats_ref[0:1, cols] = top
+    stats_ref[1:2, cols] = jnp.sum(jnp.exp(scores - top), axis=0, keepdims=True)
+
+
+def tile_kernel(
+    count, all_pairs, all_comps, e_ref, w_ref, resp_ref, loglik_ref, logw_ref,
+    hi_a, lo_a, left_a, hi_b, lo_b, left_b, scores_ref, stats_ref,
     other_ref, mine_ref, slots_ref, pair_sems, send_sems, recv_sems,
 ):
     chip, core = lax.axis_index("pairs"), lax.axis_index("comp")
@@ -336,6 +386,17 @@
         return 0
 
     lax.fori_loop(1, count, greet, 0)
+    tiles = e_ref.shape[1] // TILE
+    build_tile(0, e_ref, w_ref, hi_a, lo_a, left_a)
+
+    def two_tiles(s, _):
+        score_tile(2 * s, hi_a, lo_a, left_a, scores_ref, stats_ref)
+        build_tile(2 * s + 1, e_ref, w_ref, hi_b, lo_b, left_b)
+        score_tile(2 * s + 1, hi_b, lo_b, left_b, scores_ref, stats_ref)
+        build_tile((2 * s + 2) % tiles, e_ref, w_ref, hi_a, lo_a, left_a)
+        return 0
+
+    lax.fori_loop(0, tiles // 2, two_tiles, 0)
     pl.semaphore_wait(barrier, count)
     swap = pltpu.make_async_remote_copy(
         src_ref=stats_ref, dst_ref=other_ref, send_sem=pair_sems.at[0], recv_sem=pair_sems.at[1],
@@ -357,7 +418,7 @@
             mass = mass + resp[:, j * 128 : (j + 1) * 128]
         return mass
 
-    mass = lax.fori_loop(0, scores_ref.shape[1] // TILE, one_part, jnp.zeros((128, 128), jnp.float32))
+    mass = lax.fori_loop(0, tiles, one_part, jnp.zeros((128, 128), jnp.float32))
     own = jnp.sum(mass.T, axis=0, keepdims=True)
     mine_ref[...] = own
     slots_ref[chip] = own
@@ -380,10 +441,10 @@
         return 0
 
     lax.fori_loop(1, count, receive, 0)
-    masses = slots_ref[0]
-    for n in range(1, count):
-        masses = masses + slots_ref[n]
-    logw_ref[...] = jnp.log((masses + 1.0) / (all_pairs + all_comps))
+    parts = [slots_ref[n] for n in range(count)]
+    while len(parts) > 1:
+        parts = [parts[n] + parts[n + 1] for n in range(0, len(parts), 2)]
+    logw_ref[...] = jnp.log((parts[0] + 1.0) / (all_pairs + all_comps))
 
     def sent(d, _):
         copy_to((chip + d) % count, chip).wait_send()
@@ -392,62 +453,35 @@
     lax.fori_loop(1, count, sent, 0)
 
 
-def score_stage(effects, se_table, se_index, base_root, grid_scale, comp_base, comp_grid, weights):
-    pairs = effects.shape[1]
-    comps = comp_base.shape[0]
-    tiles = pairs // TILE
-    vmem = pl.BlockSpec(memory_space=pltpu.VMEM)
-    smem = pl.BlockSpec(memory_space=pltpu.SMEM)
-    return pl.pallas_call(
-        score_kernel,
-        grid=(tiles,),
-        in_specs=[pl.BlockSpec((R, TILE), lambda t: (0, t)), vmem, smem, vmem, smem, vmem, vmem, vmem],
-        out_specs=[vmem, pl.BlockSpec((2, TILE), lambda t: (0, t))],
-        out_shape=[
-            pltpu.VMEM((comps, pairs), jnp.float32),
-            jax.ShapeDtypeStruct((2, pairs), jnp.float32),
-        ],
-        scratch_shapes=[
-            pltpu.VMEM((R, 56, comps), jnp.float32),
-            pltpu.VMEM((R, tiles, comps), jnp.float32),
-            pltpu.VMEM((base_root.shape[0] * 56, 128), jnp.float32),
-            pltpu.VMEM((tiles, 128), jnp.float32),
-            pltpu.VMEM((2 * FEATS * 8, 128), jnp.float32),
-            pltpu.VMEM((2 * NBLK * 64 * 8, 128), jnp.float32),
-            pltpu.VMEM((2 * NBLK * 64 * 8, 128), jnp.float32),
-            pltpu.VMEM((2 * NBLK * 64 * 8, 128), jnp.float32),
-            pltpu.VMEM((2 * 64 * 8, 128), jnp.float32),
-            pltpu.VMEM((2 * 72 * 8, 128), jnp.float32),
-            pltpu.VMEM((FEATS, TILE), jnp.bfloat16),
-            pltpu.VMEM((FEATS, TILE), jnp.bfloat16),
-            pltpu.VMEM((256, FEATS), jnp.bfloat16),
-        ],
-        compiler_params=pltpu.CompilerParams(vmem_limit_bytes=44 * 1024 * 1024),
-        name="scores",
-    )(
-        effects, se_table, se_index, base_root, grid_scale,
-        comp_base.reshape(1, comps), comp_grid.reshape(1, comps), weights.reshape(1, comps),
-    )
+def write_kernel(resp_ref, loglik_ref, logw_ref, resp_out, loglik_out, logw_out, sems):
+    pairs = ((resp_ref, resp_out), (loglik_ref, loglik_out), (logw_ref, logw_out))
+    copies = [pltpu.make_async_copy(a, b, sems.at[n]) for n, (a, b) in enumerate(pairs)]
+    for copy in copies:
+        copy.start()
+    for copy in copies:
+        copy.wait()
 
 
 def per_device(effects, se_table, se_index, base_root, grid_scale, comp_base, comp_grid, weights):
     pairs = effects.shape[1]
     comps = comp_base.shape[0]
-    scores, stats = score_stage(
-        effects, se_table, se_index, base_root, grid_scale, comp_base, comp_grid, weights
-    )
+    w = sweep_stage(se_table, se_index, base_root, grid_scale, comp_base, comp_grid, weights)
     count = lax.axis_size("pairs")
     vmem = pl.BlockSpec(memory_space=pltpu.VMEM)
-    resp, loglik, logw = pl.pallas_call(
-        functools.partial(tail_kernel, count, pairs * count, comps * lax.axis_size("comp")),
+    products = [
+        pltpu.VMEM((FEATS, TILE), jnp.bfloat16),
+        pltpu.VMEM((FEATS, TILE), jnp.bfloat16),
+        pltpu.VMEM((256, FEATS), jnp.bfloat16),
+    ]
+    shapes = ((comps, pairs), (1, pairs), (1, comps))
+    results = pl.pallas_call(
+        functools.partial(tile_kernel, count, pairs * count, comps * lax.axis_size("comp")),
         in_specs=[vmem, vmem],
         out_specs=[vmem, vmem, vmem],
-        out_shape=[
+        out_shape=[pltpu.VMEM(shape, jnp.float32) for shape in shapes],
+        scratch_shapes=products + products + [
             pltpu.VMEM((comps, pairs), jnp.float32),
-            jax.ShapeDtypeStruct((1, pairs), jnp.float32),
-            jax.ShapeDtypeStruct((1, comps), jnp.float32),
-        ],
-        scratch_shapes=[
+            pltpu.VMEM((2, pairs), jnp.float32),
             pltpu.VMEM((2, pairs), jnp.float32),
             pltpu.VMEM((1, comps), jnp.float32),
             pltpu.VMEM((count, 1, comps), jnp.float32),
@@ -458,8 +492,17 @@
         compiler_params=pltpu.CompilerParams(
             collective_id=0, has_side_effects=True, vmem_limit_bytes=24 * 1024 * 1024
         ),
-        name="tail",
-    )(scores, stats)
+        name="tiles",
+    )(effects, w)
+    resp, loglik, logw = pl.pallas_call(
+        write_kernel,
+        in_specs=[vmem, vmem, vmem],
+        out_specs=[pl.BlockSpec(memory_space=pltpu.HBM)] * 3,
+        out_shape=[jax.ShapeDtypeStruct(shape, jnp.float32) for shape in shapes],
+        scratch_shapes=[pltpu.SemaphoreType.DMA((3,))],
+        compiler_params=pltpu.CompilerParams(vmem_limit_bytes=4 * 1024 * 1024),
+        name="write",
+    )(*results)
     return (resp, logw.reshape(comps), loglik.reshape(pairs))
 
 

time: 87.2 us -> 82.7 us (0.948)
  local copies, waits for them, and re-layouts: 9.74 us -> 4.97 us
    unnamed x18 -> x16, local copies, waits for them, and re-layouts: 9.74 us -> 4.97 us
    pallas_call x2 -> x3, Pallas kernels: 76.2 us -> 76.5 us  [the longest x1 43.3 us: sweep_stage(): pl.pallas_call(sweep_kernel, in_specs=[pl.BlockSpec(memory_space=pltpu.HB...]
where the time goes in v3:
time: 82.7 us; the launch traced here: 82.1 us
  Pallas kernels  76.5 us (93%)
  local copies, waits for them, and re-layouts  4.97 us (6%)
    pallas_call x1, Pallas kernels, sweep_stage(): pl.pallas_call(sweep_kernel, in_specs=[pl.BlockSpec(memory_space=pltpu.HB...  43.3 us
    pallas_call x1, Pallas kernels, per_device(): pl.pallas_call(functools.partial(tile_kernel, count, pairs * count, comps...  31.1 us
    unnamed x16, local copies, waits for them, and re-layouts  4.97 us
    pallas_call x1, Pallas kernels, per_device(): pl.pallas_call(write_kernel, in_specs=[vmem, vmem, vmem], out_specs=[pl.B...  2.05 us

profile of v3, /device:TPU:0, one launch (start us, length us, event | category | flops | bytes accessed | tf_op | source)
XLA Modules:
  0.0 82.1 jit_solution(8718776798320125154)
XLA Ops:
  0.6 0.0 copy-start.1
  0.6 1.0 %copy-done.1 = f32[16,49,49]{2,0,1:T(8,128)S(1)} copy-done((f32[16,49,49]{2,0,1:T(8,128)S(1)}, f32[16,49,49]{2,0,1:T(8,128)}, u32[]{:S(2)}) %copy-start.1) | copy-done | bytes 153688
  1.6 0.0 copy-start.2
  1.6 0.7 copy-done.2
  2.3 0.0 copy-start.3
  2.3 0.7 copy-done.3
  3.0 0.0 copy-start.4
  3.0 0.7 copy-done.4
  3.6 0.0 copy-start.5
  3.6 0.7 copy-done.5
  4.3 0.0 copy-start.6
  4.3 0.7 copy-done.6
  5.0 0.0 copy-start.7
  5.0 0.7 copy-done.7
  5.6 0.0 copy-start
  5.6 43.3 %sweep.1.w_ref = f32[20480,128]{1,0:T(8,128)S(1)} custom-call(f32[16,49]{1,0:T(8,128)S(1)} %copy-done.2, s32[16]{0:T(128)S(1)} %copy-done.3, f32[49,16,49]{2,1,0:T(8,128)S(1)} %bitcast.6, f32[16]{0:T(128)S(1)} %copy-done.4, s32[1,128]{1,0:T(1,128)S(1)} %bitcast.7, s32[1,128]{1,0:T(1,128)S(1)} %bitcast.8, f32[1,128]{1,0:T(1,128)S(1)} %bitcast.9), custom_call_target="tpu_custom_call" | custom-call | flops 250000000 | bytes 60000000 | tf_op jit(solution)/shard_map/sweep/pallas_call | solution.py:320
  49.0 0.0 copy-done
  49.0 31.1 %tiles.1 = (f32[128,8192]{1,0:T(8,128)S(1)}, f32[1,8192]{1,0:T(1,128)S(1)}, f32[1,128]{1,0:T(1,128)S(1)}) custom-call(f32[49,8192]{1,0:T(8,128)S(1)} %copy-done, f32[20480,128]{1,0:T(8,128)S(1)} %sweep.1.w_ref), custom_call_target="tpu_custom_call" | custom-call | tf_op jit(solution)/shard_map/tiles/pallas_call | solution.py:477
  80.1 2.0 %write.1 = (f32[128,8192]{1,0:T(8,128)}, f32[1,8192]{1,0:T(1,128)}, f32[1,128]{1,0:T(1,128)}) custom-call(f32[128,8192]{1,0:T(8,128)S(1)} %get-tuple-element.9.resp_ref, f32[1,8192]{1,0:T(1,128)S(1)} %get-tuple-element.10.loglik_ref, f32[1,128]{1,0:T(1,128)S(1)} %get-tuple-element.11.logw_ref), custom_call_target="tpu_custom_call" | custom-call | tf_op jit(solution)/shard_map/write/pallas_call | solution.py:497
Async XLA Ops:
  0.6 1.0 %copy-start.1 = (f32[16,49,49]{2,0,1:T(8,128)S(1)}, f32[16,49,49]{2,0,1:T(8,128)}, u32[]{:S(2)}) copy-start(f32[16,49,49]{2,0,1:T(8,128)} %param.11) | copy-start | bytes 460996
  1.6 0.7 copy-start.2
  2.3 0.7 copy-start.3
  3.0 0.7 copy-start.4
  3.6 0.7 copy-start.5
  4.3 0.7 copy-start.6
  5.0 0.7 copy-start.7
  5.6 43.3 %copy-start = (f32[49,8192]{1,0:T(8,128)S(1)}, f32[49,8192]{1,0:T(8,128)}, u32[]{:S(2)}) copy-start(f32[49,8192]{1,0:T(8,128)} %e_ref.1) | copy-start | bytes 4816900
